TPU v7x, 32 devices: a whole 2x2x4 slice. The times are simulated.
32 devices in a mesh: ka: 4 (over z), row: 8 (over y, x, core).
Axes of the slice: x: 2, y: 2, z: 4, core: 2. Of those that a mesh axis runs over, the one named last changes fastest.
Arguments:
- hamiltonian: float32 [16384, 4096], P(('ka', 'row')), parts along dimension 0, as said below
Outputs:
- sign_next: float32 [16384, 4096], P(('ka', 'row')), parts along dimension 0
- occupation: float32 [4], P('ka'), parts along dimension 0
There are 4 independent parts, one for each index of `ka`. A program takes and returns all parts, laid end to end along the dimension named above; each array names one. Nothing has to cross between parts.
Inputs may be any that keep to these rules, and one draw needn't show every extreme that they name: hamiltonian is symmetric up to float32 rounding.
All inputs are finite; a program needn't handle non-finite values.
Results may differ from a plain program's by a relative error of at most 0.0038.
Values may be sent and summed in bfloat16 or wider, within the bound.
A program may use at most 128 MiB of HBM per device.

v0:
```python
from functools import partial
import jax
import jax.numpy as jnp
from jax import lax
from jax.sharding import PartitionSpec as P


def multiply_rows(left, gathered):
    return jnp.dot(left, gathered, preferred_element_type=jnp.float32)


def own_diagonal(matrix, position, block_rows, cycle_size):
    shaped = matrix.reshape(block_rows, cycle_size, block_rows)
    square_block = lax.dynamic_slice_in_dim(shaped, position, 1, 1)[:, 0, :]
    return jnp.sum(jnp.diagonal(square_block))


def shards(hamiltonian):
    cycle_size = lax.axis_size("row")
    position = lax.axis_index("row")
    block_rows, order = hamiltonian.shape
    rounded = hamiltonian.astype(jnp.bfloat16)
    gathered = lax.all_gather(rounded, "row", axis=0, tiled=True)
    multiply = partial(multiply_rows, gathered=gathered)
    square_low = multiply(rounded).astype(jnp.bfloat16)
    cube = multiply(square_low)
    sign_next = 1.5 * hamiltonian - 0.5 * cube
    total = lax.psum(own_diagonal(sign_next, position, block_rows, cycle_size), "row")
    occupation = jnp.reshape(0.5 - total / (2.0 * order), (1,))
    return (sign_next, occupation)


def solution(mesh):
    placed = (P(("ka", "row"), None),)
    return jax.shard_map(
        shards,
        mesh=mesh,
        in_specs=placed,
        out_specs=(P(("ka", "row"), None), P("ka")),
        check_vma=False,
    )
```

profile of v0, /device:TPU:0, one launch (start us, length us, event | category | flops | bytes accessed | tf_op | source)
XLA Modules:
  0.0 269.6 jit_solution(1665986670191946976)
XLA Ops:
  7.2 0.0 all-gather.2.cloned.1.call-start
  7.2 6.0 %convert_element_type.6 = bf16[512,4096]{1,0:T(8,128)(2,1)} convert(f32[512,4096]{1,0:T(8,128)} %param.1) | non-fusion elementwise | flops 2097152 | bytes 12582912 | tf_op jit(solution)/shard_map/convert_element_type | solution.py:22
  13.2 0.0 all-gather.2.cloned.1.call-update
  13.3 163.5 %all-gather.2.cloned.1.call-done = bf16[4096,4096]{1,0:T(8,128)(2,1)} async-done(((bf16[512,4096]{1,0:T(8,128)(2,1)}), bf16[4096,4096]{1,0:T(8,128)(2,1)}) %all-gather.2.cloned.1.call-update) | async-done | bytes 33554448 | tf_op jit(solution)/shard_map/all_gather | solution.py:23
  176.8 24.8 %convolution_convert_fusion.clone.4 = bf16[512,4096]{1,0:T(8,128)(2,1)} fusion(bf16[4096,4096]{1,0:T(8,128)(2,1)} %all-gather.2.cloned.1.call-done, f32[512,4096]{1,0:T(8,128)} %param.1), kind=kOutput, calls=%fused_computation.2.clone.clone.clone.1 | convolution fusion | flops 17184063488 | bytes 46137344 | tf_op jit(solution)/shard_map/dot_general | solution.py:9
  201.6 27.9 %multiply_subtract_fusion = f32[512,4096]{1,0:T(8,128)} fusion(f32[512,4096]{1,0:T(8,128)} %param.1, bf16[4096,4096]{1,0:T(8,128)(2,1)} %all-gather.2.cloned.1.call-done, bf16[512,4096]{1,0:T(8,128)(2,1)} %convolution_convert_fusion.clone.4), kind=kOutput, calls=%fused_computation.1 | convolution fusion | flops 17186160640 | bytes 54525952 | tf_op jit(solution)/shard_map/dot_general | solution.py:9
  229.5 11.5 %copy.4 = f32[64,8,8,512]{3,2,1,0:T(8,128)S(1)} copy(f32[64,8,8,512]{3,1,2,0:T(8,128)} %bitcast.17) | data formatting | bytes 16777216
  241.0 1.1 constant_dynamic-slice_fusion
  242.1 0.1 copy.6
  242.1 4.5 %gather_fusion = f32[512]{0:T(512)S(1)} fusion(f32[512,512]{1,0:T(8,128)S(1)} %bitcast.16, s32[512]{0:T(512)S(1)} %bitcast.14), kind=kCustom, calls=%fused_computation | custom fusion | bytes 8192 | tf_op jit(solution)/shard_map/jit(diagonal)/cond/branch_0_fun/gather | solution.py:15
  246.7 0.6 reduce_sum.9
  247.3 13.7 %psum.7 = f32[]{:T(128)} all-reduce(f32[]{:T(128)} %reduce_sum.9), channel_id=1, replica_groups=mesh['ka'=4,'row'=8] {'row'}, use_global_device_ids=true, to_apply=%region_1.2 | all-reduce | flops 1 | bytes 8 | tf_op jit(solution)/shard_map/psum | solution.py:28
  (1 shorter events, 0.0 us)
Async XLA Ops:
  7.2 169.6 %all-gather.2.cloned.1.call-start = ((), (), s32[]{:S(2)}) async-start(), calls=%async_computation | async-start | bytes 37748736 | tf_op jit(solution)/shard_map/all_gather | solution.py:23
Sparse Core Ops, SparseCore 0:
  13.4 163.3 all-gather.1
where the time goes:
time: 270 us
  waiting for transfers between devices  164 us (61%)
  matrix products  52.7 us (20%)
  local copies, waits for them, and re-layouts  17.1 us (6%)
  between operations  15.8 us (6%)
  blocking collectives  13.7 us (5%)
  other arithmetic  6.63 us (2%)
    all_gather x1, waiting for transfers between devices, shards(): gathered = lax.all_gather(rounded, 'row', axis=0, tiled=True)  164 us
    dot_general x2, matrix products, multiply_rows(): return jnp.dot(left, gathered, preferred_element_type=jnp.float32)  52.7 us
    psum x1, blocking collectives, shards(): lax.psum(own_diagonal(sign_next, position, block_rows, cycle_size), 'row')  13.7 us
    unnamed x2, local copies, waits for them, and re-layouts  11.6 us
    convert_element_type x1, other arithmetic, shards(): rounded = hamiltonian.astype(jnp.bfloat16)  6.03 us
  transfers between devices with their start and end apart: 1, of which 1 were waited for; matrix products, arithmetic and copies ran while one was open for 0% of the time, Pallas kernels for 0%

commit v1 on v0

--- a/solution.py
+++ b/solution.py
@@ -25,7 +25,9 @@
     square_low = multiply(rounded).astype(jnp.bfloat16)
     cube = multiply(square_low)
     sign_next = 1.5 * hamiltonian - 0.5 * cube
-    total = lax.psum(own_diagonal(sign_next, position, block_rows, cycle_size), "row")
+    total = jnp.sum(
+        lax.all_gather(own_diagonal(sign_next, position, block_rows, cycle_size), "row"), axis=0
+    )
     occupation = jnp.reshape(0.5 - total / (2.0 * order), (1,))
     return (sign_next, occupation)
 

time: 270 us -> 271 us (level)
    psum x1 -> x0, blocking collectives: 13.7 us -> none  [shards(): lax.psum(own_diagonal(sign_next, position, block_rows, cycle_size), 'row')]
    unnamed x0 -> x1, blocking collectives: none -> 13.1 us
    unnamed x2 -> x7, local copies, waits for them, and re-layouts: 11.6 us -> 13.5 us
where the time goes in v1:
time: 271 us
  waiting for transfers between devices  163 us (60%)
  matrix products  52.7 us (19%)
  local copies, waits for them, and re-layouts  19.1 us (7%)
  between operations  15.9 us (6%)
  blocking collectives  13.1 us (5%)
  other arithmetic  7.24 us (3%)
    all_gather x1, waiting for transfers between devices, shards(): gathered = lax.all_gather(rounded, 'row', axis=0, tiled=True)  163 us
    dot_general x2, matrix products, multiply_rows(): return jnp.dot(left, gathered, preferred_element_type=jnp.float32)  52.7 us
    unnamed x7, local copies, waits for them, and re-layouts  13.5 us
    unnamed x1, blocking collectives  13.1 us
    convert_element_type x1, other arithmetic, shards(): rounded = hamiltonian.astype(jnp.bfloat16)  6.03 us
  transfers between devices with their start and end apart: 1, of which 1 were waited for; matrix products, arithmetic and copies ran while one was open for 0% of the time, Pallas kernels for 0%

profile of v1, /device:TPU:0, one launch (start us, length us, event | category | flops | bytes accessed | tf_op | source)
XLA Modules:
  0.0 271.0 jit_solution(15970928438815267318)
XLA Ops:
  7.2 0.0 copy-start
  7.2 0.0 all-gather.2.cloned.1.call-start
  7.2 6.0 %convert_element_type.6 = bf16[512,4096]{1,0:T(8,128)(2,1)} convert(f32[512,4096]{1,0:T(8,128)} %param.1) | non-fusion elementwise | flops 2097152 | bytes 12582912 | tf_op jit(solution)/shard_map/convert_element_type | solution.py:22
  13.2 0.0 all-gather.2.cloned.1.call-update
  13.3 0.0 copy-done
  13.3 0.6 dynamic-slice
  13.9 162.9 %all-gather.2.cloned.1.call-done = bf16[4096,4096]{1,0:T(8,128)(2,1)} async-done(((bf16[512,4096]{1,0:T(8,128)(2,1)}), bf16[4096,4096]{1,0:T(8,128)(2,1)}) %all-gather.2.cloned.1.call-update) | async-done | bytes 33554448 | tf_op jit(solution)/shard_map/all_gather | solution.py:23
  176.8 24.8 %convolution_convert_fusion.clone.4 = bf16[512,4096]{1,0:T(8,128)(2,1)} fusion(bf16[4096,4096]{1,0:T(8,128)(2,1)} %all-gather.2.cloned.1.call-done, f32[512,4096]{1,0:T(8,128)} %param.1), kind=kOutput, calls=%fused_computation.2.clone.clone.clone.1 | convolution fusion | flops 17184063488 | bytes 46137344 | tf_op jit(solution)/shard_map/dot_general | solution.py:9
  201.6 27.9 %multiply_subtract_fusion = f32[512,4096]{1,0:T(8,128)} fusion(f32[512,4096]{1,0:T(8,128)} %param.1, bf16[4096,4096]{1,0:T(8,128)(2,1)} %all-gather.2.cloned.1.call-done, bf16[512,4096]{1,0:T(8,128)(2,1)} %convolution_convert_fusion.clone.4), kind=kOutput, calls=%fused_computation.1 | convolution fusion | flops 17186160640 | bytes 54525952 | tf_op jit(solution)/shard_map/dot_general | solution.py:9
  229.5 11.5 %copy.4 = f32[64,8,8,512]{3,2,1,0:T(8,128)S(1)} copy(f32[64,8,8,512]{3,1,2,0:T(8,128)} %bitcast.19) | data formatting | bytes 16777216
  241.0 1.1 constant_dynamic-slice_fusion
  242.1 0.1 copy.6
  242.1 4.5 %gather_fusion = f32[512]{0:T(512)S(1)} fusion(f32[512,512]{1,0:T(8,128)S(1)} %bitcast.18, s32[512]{0:T(512)S(1)} %bitcast.16), kind=kCustom, calls=%fused_computation | custom fusion | bytes 8192 | tf_op jit(solution)/shard_map/jit(diagonal)/cond/branch_0_fun/gather | solution.py:15
  246.7 0.6 reduce_sum.18
  247.3 1.4 dynamic-update-slice
  248.7 13.1 %all-reduce = f32[8]{0:T(128)S(1)} all-reduce(f32[8]{0:T(128)S(1)} %dynamic-update-slice), channel_id=1, replica_groups=mesh['ka'=4,'row'=8] {'row'}, use_global_device_ids=true, to_apply=%add | all-reduce | flops 8 | bytes 64
  261.7 0.6 reduce_sum.19
  (2 shorter events, 0.0 us)
Async XLA Ops:
  7.2 6.1 %copy-start = (u32[32]{0:T(128)S(1)}, u32[32]{0:T(128)}, u32[]{:S(2)}) copy-start(u32[32]{0:T(128)} %constant.38) | copy-start | bytes 388
  7.2 169.6 %all-gather.2.cloned.1.call-start = ((), (), s32[]{:S(2)}) async-start(), calls=%async_computation | async-start | bytes 37748736 | tf_op jit(solution)/shard_map/all_gather | solution.py:23
Sparse Core Ops, SparseCore 0:
  13.4 163.3 all-gather.1

commit v2 on v0

--- a/solution.py
+++ b/solution.py
@@ -3,6 +3,27 @@
 import jax.numpy as jnp
 from jax import lax
 from jax.sharding import PartitionSpec as P
+
+
+def ring_gather(array, axis, dim):
+    size, index, rows = (lax.axis_size(axis), lax.axis_index(axis), array.shape[dim])
+    ahead = [(i, (i + 1) % size) for i in range(size)]
+    left = [(i, (i - 1) % size) for i in range(size)]
+    out = jnp.zeros((*array.shape[:dim], size * rows, *array.shape[dim + 1 :]), array.dtype)
+    out = lax.dynamic_update_slice_in_dim(out, array, index * rows, axis=dim)
+    from_left = from_right = array
+    halfway = size // 2
+    for step in range(1, halfway + 1):
+        from_left = lax.ppermute(from_left, axis, ahead)
+        out = lax.dynamic_update_slice_in_dim(
+            out, from_left, (index - step) % size * rows, axis=dim
+        )
+        if step < size - halfway:
+            from_right = lax.ppermute(from_right, axis, left)
+            out = lax.dynamic_update_slice_in_dim(
+                out, from_right, (index + step) % size * rows, axis=dim
+            )
+    return out
 
 
 def multiply_rows(left, gathered):
@@ -20,7 +41,7 @@
     position = lax.axis_index("row")
     block_rows, order = hamiltonian.shape
     rounded = hamiltonian.astype(jnp.bfloat16)
-    gathered = lax.all_gather(rounded, "row", axis=0, tiled=True)
+    gathered = ring_gather(rounded, "row", 0)
     multiply = partial(multiply_rows, gathered=gathered)
     square_low = multiply(rounded).astype(jnp.bfloat16)
     cube = multiply(square_low)

time: 270 us -> 435 us (1.61)
  waiting for transfers between devices: 164 us -> 288 us
  local copies, waits for them, and re-layouts: 17.1 us -> 60.2 us
  between operations: 15.8 us -> 2.48 us
  starting transfers between devices: 0.04 us -> 9.34 us
    ppermute x0 -> x7, waiting for transfers between devices: none -> 288 us  [the longest x4 284 us: ring_gather(): from_left = lax.ppermute(from_left, axis, ahead)]
    all_gather x1 -> x0, waiting for transfers between devices: 164 us -> none  [shards(): gathered = lax.all_gather(rounded, 'row', axis=0, tiled=True)]
    dynamic_update_slice x0 -> x7, local copies, waits for them, and re-layouts: none -> 28.2 us  [the longest x4 16.5 us: ring_gather(): lax.dynamic_update_slice_in_dim(out, from_left, (index - step) % size * r...]
    broadcast_in_dim x0 -> x1, local copies, waits for them, and re-layouts: none -> 13.1 us  [ring_gather(): jnp.zeros((*array.shape[:dim], size * rows, *array.shape[dim + 1:]), arra...]
    ppermute x0 -> x7, starting transfers between devices: none -> 9.34 us  [the longest x3 8.82 us: ring_gather(): from_right = lax.ppermute(from_right, axis, left)]
    convert_element_type x1 -> x0, other arithmetic: 6.03 us -> none  [shards(): rounded = hamiltonian.astype(jnp.bfloat16)]
    unnamed x2 -> x18, local copies, waits for them, and re-layouts: 11.6 us -> 13.4 us
  transfers between devices with their start and end apart: 1 -> 7, of which waited for: 1 -> 6; matrix products, arithmetic and copies ran while one was open for 0% -> 5% of each run, Pallas kernels for 0% -> 0%
where the time goes in v2:
time: 435 us; the launch traced here: 433 us
  waiting for transfers between devices  288 us (66%)
  local copies, waits for them, and re-layouts  60.2 us (14%)
  matrix products  52.4 us (12%)
  blocking collectives  17.1 us (4%)
  starting transfers between devices  9.34 us (2%)
    ppermute x4, waiting for transfers between devices, ring_gather(): from_left = lax.ppermute(from_left, axis, ahead)  284 us
    dot_general x2, matrix products, multiply_rows(): return jnp.dot(left, gathered, preferred_element_type=jnp.float32)  52.4 us
    psum x1, blocking collectives, shards(): lax.psum(own_diagonal(sign_next, position, block_rows, cycle_size), 'row')  17.1 us
    dynamic_update_slice x4, local copies, waits for them, and re-layouts, ring_gather(): lax.dynamic_update_slice_in_dim(out, from_left, (index - step) % size * r...  16.5 us
    unnamed x18, local copies, waits for them, and re-layouts  13.4 us
    broadcast_in_dim x1, local copies, waits for them, and re-layouts, ring_gather(): jnp.zeros((*array.shape[:dim], size * rows, *array.shape[dim + 1:]), arra...  13.1 us
    dynamic_update_slice x3, local copies, waits for them, and re-layouts, ring_gather(): lax.dynamic_update_slice_in_dim(out, from_right, (index + step) % size *...  11.7 us
    ppermute x3, starting transfers between devices, ring_gather(): from_right = lax.ppermute(from_right, axis, left)  8.82 us
  transfers between devices with their start and end apart: 7, of which 6 were waited for; matrix products, arithmetic and copies ran while one was open for 5% of the time, Pallas kernels for 0%

profile of v2, /device:TPU:0, one launch (start us, length us, event | category | flops | bytes accessed | tf_op | source)
XLA Modules:
  0.0 433.1 jit_solution(2639512010136268924)
XLA Ops:
  0.6 0.0 copy-start
  0.6 13.1 %broadcast_in_dim.7 = bf16[4096,4096]{1,0:T(8,128)(2,1)} broadcast(bf16[]{:T(256)} %constant.61.clone.1), dimensions={} | broadcast | bytes 33554432 | tf_op jit(solution)/shard_map/broadcast_in_dim | solution.py:12
  13.7 0.0 copy-done
  13.7 3.0 constant_dynamic-update-slice_fusion.7
  16.7 0.0 copy-start.1
  16.7 0.5 collective-permute-start
  17.2 1.5 copy-done.1
  18.8 3.3 collective-permute-start.1
  22.1 86.1 %collective-permute-done = bf16[512,4096]{1,0:T(8,128)(2,1)S(1)} collective-permute-done((bf16[512,4096]{1,0:T(8,128)(2,1)S(1)}, bf16[512,4096]{1,0:T(8,128)(2,1)S(1)}, u32[]{:S(2)}, u32[]{:S(2)}) %collective-permute-start) | collective-permute-done | bytes 4194336 | tf_op jit(solution)/shard_map/ppermute | solution.py:17
  108.2 0.0 copy-start.3
  108.2 0.0 collective-permute-start.2
  108.2 1.9 collective-permute-done.1
  110.1 0.2 copy-done.3
  110.2 0.0 copy-start.4
  110.2 2.7 collective-permute-start.3
  112.9 86.1 %collective-permute-done.2 = bf16[512,4096]{1,0:T(8,128)(2,1)S(1)} collective-permute-done((bf16[512,4096]{1,0:T(8,128)(2,1)S(1)}, bf16[512,4096]{1,0:T(8,128)(2,1)S(1)}, u32[]{:S(2)}, u32[]{:S(2)}) %collective-permute-start.2) | collective-permute-done | bytes 4194336 | tf_op jit(solution)/shard_map/ppermute | solution.py:17
  199.0 0.0 copy-done.4
  199.0 0.0 copy-start.6
  199.0 0.0 collective-permute-start.4
  199.0 1.9 collective-permute-done.3
  200.9 0.1 copy-done.6
  201.0 2.8 collective-permute-start.5
  203.8 86.5 %collective-permute-done.4 = bf16[512,4096]{1,0:T(8,128)(2,1)} collective-permute-done((bf16[512,4096]{1,0:T(8,128)(2,1)S(1)}, bf16[512,4096]{1,0:T(8,128)(2,1)}, u32[]{:S(2)}, u32[]{:S(2)}) %collective-permute-start.4) | collective-permute-done | bytes 4194336 | tf_op jit(solution)/shard_map/ppermute | solution.py:17
  290.3 0.0 collective-permute-start.6
  290.3 0.0 copy-start.5
  290.3 0.0 copy-start.7
  290.3 5.0 %constant_dynamic-update-slice_fusion.6 = bf16[4096,4096]{1,0:T(8,128)(2,1)} fusion(bf16[4096,4096]{1,0:T(8,128)(2,1)} %get-tuple-element.2, bf16[512,4096]{1,0:T(8,128)(2,1)} %copy-done.3, s32[]{:T(128)S(6)} %select_n.64), kind=kLoop, calls=%fused_computation.11 | loop fusion | bytes 8388612 | tf_op jit(solution)/shard_map/dynamic_update_slice | solution.py:18
  295.3 0.0 copy-done.5
  295.3 2.2 constant_dynamic-update-slice_fusion.5
  297.5 0.0 copy-done.7
  297.6 2.2 constant_dynamic-update-slice_fusion.4
  299.8 4.7 %constant_dynamic-update-slice_fusion.3 = bf16[4096,4096]{1,0:T(8,128)(2,1)} fusion(bf16[4096,4096]{1,0:T(8,128)(2,1)} %constant_dynamic-update-slice_fusion.4, bf16[512,4096]{1,0:T(8,128)(2,1)} %collective-permute-done.3, s32[]{:T(128)S(6)} %select_n.70), kind=kLoop, calls=%fused_computation.8 | loop fusion | bytes 8388612 | tf_op jit(solution)/shard_map/dynamic_update_slice | solution.py:23
  304.4 4.7 %constant_dynamic-update-slice_fusion.2 = bf16[4096,4096]{1,0:T(8,128)(2,1)} fusion(bf16[4096,4096]{1,0:T(8,128)(2,1)} %constant_dynamic-update-slice_fusion.3, bf16[512,4096]{1,0:T(8,128)(2,1)} %collective-permute-done.4, s32[]{:T(128)S(6)} %select_n.72), kind=kLoop, calls=%fused_computation.7 | loop fusion | bytes 8388612 | tf_op jit(solution)/shard_map/dynamic_update_slice | solution.py:18
  309.1 0.0 copy-start.2
  309.1 0.0 collective-permute-done.5
  309.1 4.8 %constant_dynamic-update-slice_fusion.1 = bf16[4096,4096]{1,0:T(8,128)(2,1)} fusion(bf16[4096,4096]{1,0:T(8,128)(2,1)} %constant_dynamic-update-slice_fusion.2, bf16[512,4096]{1,0:T(8,128)(2,1)} %collective-permute-done.5, s32[]{:T(128)S(6)} %select_n.74), kind=kLoop, calls=%fused_computation.6 | loop fusion | bytes 8388612 | tf_op jit(solution)/shard_map/dynamic_update_slice | solution.py:23
  313.9 25.6 %collective-permute-done.6 = bf16[512,4096]{1,0:T(8,128)(2,1)} collective-permute-done((bf16[512,4096]{1,0:T(8,128)(2,1)}, bf16[512,4096]{1,0:T(8,128)(2,1)}, u32[]{:S(2)}, u32[]{:S(2)}) %collective-permute-start.6) | collective-permute-done | bytes 4194336 | tf_op jit(solution)/shard_map/ppermute | solution.py:17
  339.4 4.6 %constant_dynamic-update-slice_fusion = bf16[4096,4096]{1,0:T(8,128)(2,1)} fusion(bf16[4096,4096]{1,0:T(8,128)(2,1)} %constant_dynamic-update-slice_fusion.1, bf16[512,4096]{1,0:T(8,128)(2,1)} %collective-permute-done.6, s32[]{:T(128)S(6)} %select_n.76), kind=kLoop, calls=%fused_computation.5 | loop fusion | bytes 8388612 | tf_op jit(solution)/shard_map/dynamic_update_slice | solution.py:18
  344.1 0.0 copy-done.2
  344.1 24.0 %convolution_convert_fusion.clone.4 = bf16[4096,512]{1,0:T(8,128)(2,1)} fusion(bf16[4096,4096]{1,0:T(8,128)(2,1)} %constant_dynamic-update-slice_fusion, bf16[512,4096]{1,0:T(8,128)(2,1)S(1)} %copy-done.2), kind=kOutput, calls=%fused_computation.2.clone.clone.clone.1 | convolution fusion | flops 17181966336 | bytes 41943040 | tf_op jit(solution)/shard_map/dot_general | solution.py:30
  368.1 28.3 %multiply_subtract_fusion = f32[512,4096]{1,0:T(8,128)} fusion(f32[512,4096]{1,0:T(8,128)} %param.1, bf16[4096,4096]{1,0:T(8,128)(2,1)} %constant_dynamic-update-slice_fusion, bf16[4096,512]{1,0:T(8,128)(2,1)} %convolution_convert_fusion.clone.4), kind=kOutput, calls=%fused_computation.1 | convolution fusion | flops 17186160640 | bytes 54525952 | tf_op jit(solution)/shard_map/dot_general | solution.py:30
  396.4 11.5 %copy.4 = f32[64,8,8,512]{3,2,1,0:T(8,128)S(1)} copy(f32[64,8,8,512]{3,1,2,0:T(8,128)} %bitcast.21) | data formatting | bytes 16777216
  407.9 1.1 constant_dynamic-slice_fusion
  409.0 0.1 copy.6
  409.1 4.5 %gather_fusion = f32[512]{0:T(512)S(1)} fusion(f32[512,512]{1,0:T(8,128)S(1)} %bitcast.20, s32[512]{0:T(512)S(1)} %bitcast.18), kind=kCustom, calls=%fused_computation | custom fusion | bytes 8192 | tf_op jit(solution)/shard_map/jit(diagonal)/cond/branch_0_fun/gather | solution.py:36
  413.6 0.6 reduce_sum.9
  414.2 17.1 %psum.7 = f32[]{:T(128)} all-reduce(f32[]{:T(128)} %reduce_sum.9), channel_id=1, replica_groups=mesh['ka'=4,'row'=8] {'row'}, use_global_device_ids=true, to_apply=%region_1.2 | all-reduce | flops 1 | bytes 8 | tf_op jit(solution)/shard_map/psum | solution.py:49
  (1 shorter events, 0.0 us)
Async XLA Ops:
  0.6 13.1 %copy-start = (f32[512,4096]{1,0:T(8,128)S(1)}, f32[512,4096]{1,0:T(8,128)}, u32[]{:S(2)}) copy-start(f32[512,4096]{1,0:T(8,128)} %param.1) | copy-start | bytes 25165828
  16.7 2.1 copy-start.1
  16.7 91.5 %collective-permute-start = (bf16[512,4096]{1,0:T(8,128)(2,1)S(1)}, bf16[512,4096]{1,0:T(8,128)(2,1)S(1)}, u32[]{:S(2)}, u32[]{:S(2)}) collective-permute-start(bf16[512,4096]{1,0:T(8,128)(2,1)S(1)} %get-tuple-element.3), channel_id=1, source_target_pairs={{0,1},{1,2},{2,3},{3,4},{4,5},{5,6},{6,7},{7,0},{8,9},{9,10},{10,1... | collective-permute-start | bytes 12582920 | tf_op jit(solution)/shard_map/ppermute | solution.py:17
  18.8 91.3 %collective-permute-start.1 = (bf16[512,4096]{1,0:T(8,128)(2,1)S(1)}, bf16[512,4096]{1,0:T(8,128)(2,1)S(1)}, u32[]{:S(2)}, u32[]{:S(2)}) collective-permute-start(bf16[512,4096]{1,0:T(8,128)(2,1)S(1)} %get-tuple-element.3), channel_id=1, source_target_pairs={{0,7},{1,0},{2,1},{3,2},{4,3},{5,4},{6,5},{7,6},{8,15},{9,8},{10,9... | collective-permute-start | bytes 12582920 | tf_op jit(solution)/shard_map/ppermute | solution.py:22
  108.2 2.0 copy-start.3
  108.2 90.8 %collective-permute-start.2 = (bf16[512,4096]{1,0:T(8,128)(2,1)S(1)}, bf16[512,4096]{1,0:T(8,128)(2,1)S(1)}, u32[]{:S(2)}, u32[]{:S(2)}) collective-permute-start(bf16[512,4096]{1,0:T(8,128)(2,1)S(1)} %collective-permute-done), channel_id=1, source_target_pairs={{0,1},{1,2},{2,3},{3,4},{4,5},{5,6},{6,7},{7,0},{8,9},{9,10},{10,1... | collective-permute-start | bytes 12582920 | tf_op jit(solution)/shard_map/ppermute | solution.py:17
  110.2 88.8 %copy-start.4 = (bf16[512,4096]{1,0:T(8,128)(2,1)}, bf16[512,4096]{1,0:T(8,128)(2,1)S(1)}, u32[]{:S(2)}) copy-start(bf16[512,4096]{1,0:T(8,128)(2,1)S(1)} %collective-permute-done.1) | copy-start | bytes 12582916
  110.2 90.6 %collective-permute-start.3 = (bf16[512,4096]{1,0:T(8,128)(2,1)S(1)}, bf16[512,4096]{1,0:T(8,128)(2,1)}, u32[]{:S(2)}, u32[]{:S(2)}) collective-permute-start(bf16[512,4096]{1,0:T(8,128)(2,1)S(1)} %collective-permute-done.1), channel_id=1, source_target_pairs={{0,7},{1,0},{2,1},{3,2},{4,3},{5,4},{6,5},{7,6},{8,15},{9,8},{10,9... | collective-permute-start | bytes 12582920 | tf_op jit(solution)/shard_map/ppermute | solution.py:22
  199.0 2.0 copy-start.6
  199.0 91.3 %collective-permute-start.4 = (bf16[512,4096]{1,0:T(8,128)(2,1)S(1)}, bf16[512,4096]{1,0:T(8,128)(2,1)}, u32[]{:S(2)}, u32[]{:S(2)}) collective-permute-start(bf16[512,4096]{1,0:T(8,128)(2,1)S(1)} %collective-permute-done.2), channel_id=1, source_target_pairs={{0,1},{1,2},{2,3},{3,4},{4,5},{5,6},{6,7},{7,0},{8,9},{9,10},{10,1... | collective-permute-start | bytes 12582920 | tf_op jit(solution)/shard_map/ppermute | solution.py:17
  201.0 108.1 %collective-permute-start.5 = (bf16[512,4096]{1,0:T(8,128)(2,1)}, bf16[512,4096]{1,0:T(8,128)(2,1)}, u32[]{:S(2)}, u32[]{:S(2)}) collective-permute-start(bf16[512,4096]{1,0:T(8,128)(2,1)} %collective-permute-done.3), channel_id=1, source_target_pairs={{0,7},{1,0},{2,1},{3,2},{4,3},{5,4},{6,5},{7,6},{8,15},{9,8},{10,9... | collective-permute-start | bytes 12582920 | tf_op jit(solution)/shard_map/ppermute | solution.py:22
  290.3 49.1 %collective-permute-start.6 = (bf16[512,4096]{1,0:T(8,128)(2,1)}, bf16[512,4096]{1,0:T(8,128)(2,1)}, u32[]{:S(2)}, u32[]{:S(2)}) collective-permute-start(bf16[512,4096]{1,0:T(8,128)(2,1)} %collective-permute-done.4), channel_id=1, source_target_pairs={{0,1},{1,2},{2,3},{3,4},{4,5},{5,6},{6,7},{7,0},{8,9},{9,10},{10,1... | collective-permute-start | bytes 12582920 | tf_op jit(solution)/shard_map/ppermute | solution.py:17
  290.3 5.0 %copy-start.5 = (bf16[512,4096]{1,0:T(8,128)(2,1)S(1)}, bf16[512,4096]{1,0:T(8,128)(2,1)}, u32[]{:S(2)}) copy-start(bf16[512,4096]{1,0:T(8,128)(2,1)} %copy-done.4) | copy-start | bytes 12582916
  290.3 7.2 %copy-start.7 = (bf16[512,4096]{1,0:T(8,128)(2,1)S(1)}, bf16[512,4096]{1,0:T(8,128)(2,1)}, u32[]{:S(2)}) copy-start(bf16[512,4096]{1,0:T(8,128)(2,1)} %copy-done.6) | copy-start | bytes 12582916
  309.1 35.0 %copy-start.2 = (bf16[512,4096]{1,0:T(8,128)(2,1)S(1)}, bf16[512,4096]{1,0:T(8,128)(2,1)}, u32[]{:S(2)}) copy-start(bf16[512,4096]{1,0:T(8,128)(2,1)} %copy-done.1) | copy-start | bytes 12582916
